TPU v7x, 128 devices: a whole 4x4x4 slice. The times are simulated.
128 devices in a mesh: seq: 32 (over y, z_hi, x), sub: 4 (over z_lo, core).
Axes of the slice: x: 4, y: 4, z: 4 (z_hi: 2, z_lo: 2; z = z_hi * 2 + z_lo), core: 2. Of those that a mesh axis runs over, the one named last changes fastest.
Arguments:
- tokens: bfloat16 [8192, 4096], P('seq'), may hold values from -6 to 6
- w_split: bfloat16 [4096, 4096], P(None, 'sub'), may hold values from -0.09375 to 0.09375
- w_merge: bfloat16 [4096, 4096], P('sub'), may hold values from -0.09375 to 0.09375
- expert_in: bfloat16 [128, 1024, 2048], P(('seq', 'sub')), may hold values from -0.1875 to 0.1875
- expert_out: bfloat16 [128, 1024, 1024], P(('seq', 'sub')), may hold values from -0.1875 to 0.1875
- expert_ids: int32 [4, 8192, 2], P('sub', 'seq'), may hold values from 0 to 127, all different within a row; in each aligned block of 256 rows (0 to 255, 256 to 511, ..., all dimensions but the last counted through in order) at most 6 rows name the same one
- combine_q: int32 [4, 8192, 2], P('sub', 'seq'), may hold values from 4096 to 65536
- capacity: int32 [128], replicated, may hold values from 3 to 6
Outputs:
- mixed: bfloat16 [8192, 4096], P('seq', 'sub')
Inputs may be any that keep to these rules, and one draw needn't show every extreme that they name: `expert_ids`: in each block of 256 positions of one sub-head, the ids of a position differ, no expert is named more than 6 times, a bound that some block reaches.
All inputs are finite; a program needn't handle non-finite values.
Results may differ from a plain program's by a relative error of at most 0.0076.
Values may be sent and summed in bfloat16 or wider, within the bound.
A program may use at most 128 MiB of HBM per device.

v0:
```python
import jax
import jax.numpy as jnp
from jax import lax
from jax.sharding import PartitionSpec as P


def split_up(shard, dim, peers):
    lengths = shard.shape
    blocks = shard.reshape(*lengths[:dim], peers, lengths[dim] // peers, *lengths[dim + 1 :])
    return jnp.moveaxis(blocks, dim, 0)


def summed_on_arrival(shard, axis, dim):
    blocks = split_up(shard, dim, lax.axis_size(axis))
    arrived = lax.all_to_all(blocks, axis, split_axis=0, concat_axis=0, tiled=True)
    return arrived.astype(jnp.float32).sum(axis=0)


def expert_rows(received, expert_in, expert_out):
    dims_in = received.shape
    rows_flat = received.reshape(-1, dims_in[-1])
    gate_up = jnp.dot(rows_flat, expert_in[0], preferred_element_type=jnp.float32)
    ffe_width = expert_out.shape[1]
    hidden = (jax.nn.silu(gate_up[:, :ffe_width]) * gate_up[:, ffe_width:]).astype(jnp.bfloat16)
    result = jnp.dot(hidden, expert_out[0], preferred_element_type=jnp.float32).astype(jnp.bfloat16)
    return result.reshape(dims_in)


def body(tokens, w_split, w_merge, expert_in, expert_out, expert_ids, combine_q, capacity):
    sub_tok = jnp.dot(tokens, w_split, preferred_element_type=jnp.float32).astype(jnp.bfloat16)
    tok_rows = tokens.shape[0]
    experts = capacity.shape[0]
    slot_count = 3 * tok_rows // experts
    expert_of = expert_ids[0].reshape(-1)
    onehot = (expert_of[:, None] == jnp.arange(experts, dtype=jnp.int32)[None, :]).astype(jnp.int32)
    order_rank = jnp.sum((jnp.cumsum(onehot, axis=0) - onehot) * onehot, axis=1)
    cap_limit = jnp.sum(onehot * capacity[None, :], axis=1)
    is_kept = order_rank < cap_limit
    slot_index = jnp.where(is_kept, expert_of * slot_count + order_rank, -1)
    target = jnp.arange(experts * slot_count, dtype=jnp.int32)
    chosen = jnp.any(
        target[:, None, None] == slot_index.reshape(tok_rows, -1)[None, :, :], axis=2
    ).astype(jnp.bfloat16)
    packed = jnp.dot(chosen, sub_tok, preferred_element_type=jnp.float32).astype(jnp.bfloat16)
    packed = packed.reshape(experts, slot_count, -1)
    answered = expert_rows(
        lax.all_to_all(packed, ("seq", "sub"), split_axis=0, concat_axis=0, tiled=True),
        expert_in,
        expert_out,
    )
    returned_rows = lax.all_to_all(
        answered, ("seq", "sub"), split_axis=0, concat_axis=0, tiled=True
    )
    returned_rows = returned_rows.reshape(experts * slot_count, -1)
    gathered = returned_rows[jnp.maximum(slot_index, 0)].astype(jnp.float32)
    weight = jnp.where(is_kept, combine_q[0].reshape(-1).astype(jnp.float32) / 65536.0, 0.0)
    weighted = (weight[:, None] * gathered).reshape(tok_rows, -1, gathered.shape[1])
    head_out = jnp.sum(weighted, axis=1).astype(jnp.bfloat16)
    partial_value = jnp.dot(head_out, w_merge, preferred_element_type=jnp.float32)
    return summed_on_arrival(partial_value.astype(jnp.bfloat16), "sub", 1).astype(jnp.bfloat16)


def solution(mesh):
    in_specs = (
        P("seq", None),
        P(None, "sub"),
        P("sub", None),
        P(("seq", "sub"), None, None),
        P(("seq", "sub"), None, None),
        P("sub", "seq", None),
        P("sub", "seq", None),
        P(),
    )
    out_specs = P("seq", "sub")
    return jax.shard_map(body, mesh=mesh, in_specs=in_specs, out_specs=out_specs, check_vma=False)
```

profile of v0, /device:TPU:1, one launch (start us, length us, event | category | flops | bytes accessed | tf_op | source)
XLA Modules:
  0.0 160.0 jit_solution(17669332753127285432)
XLA Ops:
  0.0 0.0 copy-start
  0.0 1.0 copy.24
  1.0 0.1 eq.44
  1.1 0.1 eq.40
  1.3 0.1 copy.26
  1.4 0.2 fusion.13
  1.7 1.0 select_reduce_fusion
  2.6 0.1 reduce_sum.49
  2.8 0.1 reduce_sum.50
  3.0 0.1 copy.30
  3.1 0.3 fusion.9
  3.3 0.0 copy-done
  3.4 7.3 %convolution_convert_fusion.1 = bf16[768,1024]{1,0:T(8,128)(2,1)} fusion(pred[768,256]{1,0:T(8,128)(4,1)S(1)} %fusion.9, bf16[256,4096]{1,0:T(8,128)(2,1)S(1)} %copy-done, bf16[4096,1024]{1,0:T(8,128)(2,1)} %param.9), kind=kOutput, calls=%fused_computation.11 | convolution fusion | flops 2551185408 | bytes 12255232 | tf_op jit(solution)/shard_map/dot_general | solution.py:44
  10.6 3.7 %reshape.109 = bf16[128,6,1024]{2,1,0:T(8,128)(2,1)} reshape(bf16[768,1024]{1,0:T(8,128)(2,1)} %convolution_convert_fusion.1) | data formatting | bytes 3145728 | tf_op jit(solution)/shard_map/reshape | solution.py:45
  14.3 41.5 %all_to_all.15 = bf16[128,6,1024]{2,1,0:T(8,128)(2,1)} all-to-all(bf16[128,6,1024]{2,1,0:T(8,128)(2,1)} %reshape.109), channel_id=1, replica_groups=mesh['seq'=32,'sub'=4] {'seq','sub'}, dimensions={0} | all-to-all | bytes 3145728 | tf_op jit(solution)/shard_map/all_to_all | solution.py:47
  55.9 3.7 %reshape.110 = bf16[768,1024]{1,0:T(8,128)(2,1)} reshape(bf16[128,6,1024]{2,1,0:T(8,128)(2,1)} %all_to_all.15) | data formatting | bytes 3145728 | tf_op jit(solution)/shard_map/reshape | solution.py:21
  59.6 5.8 %fusion = f32[768,2048]{1,0:T(8,128)S(1)} fusion(bf16[768,1024]{1,0:T(8,128)(2,1)} %reshape.110, bf16[1,1024,2048]{2,1,0:T(8,128)(2,1)} %param.11), kind=kOutput, calls=%fused_computation.2 | convolution fusion | flops 3221225472 | bytes 12058624 | tf_op jit(solution)/shard_map/dot_general | solution.py:22
  65.4 3.0 %fusion.5 = bf16[768,1024]{1,0:T(8,128)(2,1)} fusion(bf16[1,1024,1024]{2,1,0:T(8,128)(2,1)S(1)} %copy-done.2, f32[768,2048]{1,0:T(8,128)S(1)} %fusion), kind=kOutput, calls=%fused_computation.10 | convolution fusion | flops 1616117760 | bytes 9961472 | tf_op jit(solution)/shard_map/dot_general | solution.py:25
  68.4 3.7 %reshape.111 = bf16[128,6,1024]{2,1,0:T(8,128)(2,1)} reshape(bf16[768,1024]{1,0:T(8,128)(2,1)} %fusion.5) | data formatting | bytes 3145728 | tf_op jit(solution)/shard_map/reshape | solution.py:26
  72.1 5.7 %all-to-all-start.1 = ((bf16[128,6,1024]{2,1,0:T(8,128)(2,1)}), bf16[128,6,1024]{2,1,0:T(8,128)(2,1)}, u32[]{:S(2)}, u32[]{:S(2)}) async-start(bf16[128,6,1024]{2,1,0:T(8,128)(2,1)} %reshape.111), calls=%async_computation.1 | async-start | bytes 4194304 | tf_op jit(solution)/shard_map/all_to_all | solution.py:51
  77.8 0.1 mul.52
  78.0 0.2 lt.29
  78.2 0.1 copy.28
  78.4 29.1 %all-to-all-done.1 = bf16[128,6,1024]{2,1,0:T(8,128)(2,1)} async-done(((bf16[128,6,1024]{2,1,0:T(8,128)(2,1)}), bf16[128,6,1024]{2,1,0:T(8,128)(2,1)}, u32[]{:S(2)}, u32[]{:S(2)}) %all-to-all-start.1) | async-done | bytes 1572896 | tf_op jit(solution)/shard_map/all_to_all | solution.py:51
  107.5 3.7 %reshape.112 = bf16[768,1024]{1,0:T(8,128)(2,1)} reshape(bf16[128,6,1024]{2,1,0:T(8,128)(2,1)} %all-to-all-done.1) | data formatting | bytes 3145728 | tf_op jit(solution)/shard_map/reshape | solution.py:54
  111.2 4.3 %gather_fusion = bf16[512,1024]{1,0:T(8,128)(2,1)S(1)} fusion(bf16[768,1024]{1,0:T(8,128)(2,1)} %reshape.112, s32[1024]{0:T(1024)S(1)} %pad_clamp_fusion), kind=kCustom, calls=%fused_computation | custom fusion | bytes 2099200 | tf_op jit(solution)/shard_map/gather | solution.py:55
  115.6 2.4 %reshape.114 = f32[256,2,1024]{2,1,0:T(2,128)} reshape(bf16[512,1024]{1,0:T(8,128)(2,1)S(1)} %gather_fusion) | data formatting | bytes 3145728 | tf_op jit(solution)/shard_map/convert_element_type | solution.py:55
  117.9 4.3 %multiply_reduce_fusion = bf16[256,1024]{1,0:T(8,128)(2,1)S(1)} fusion(f32[256,2,1024]{2,1,0:T(2,128)} %reshape.114, f32[256,2]{1,0:T(8,128)S(1)} %bitcast_select_fusion), kind=kLoop, calls=%fused_computation.9 | loop fusion | flops 786432 | bytes 2623488 | tf_op jit(solution)/shard_map/reduce_sum | solution.py:58
  122.3 5.7 %convolution_convert_fusion = bf16[256,4096]{1,0:T(8,128)(2,1)S(1)} fusion(bf16[1024,4096]{1,0:T(8,128)(2,1)} %param.10, bf16[256,1024]{1,0:T(8,128)(2,1)S(1)} %multiply_reduce_fusion), kind=kOutput, calls=%fused_computation.1 | convolution fusion | flops 2148532224 | bytes 11010048 | tf_op jit(solution)/shard_map/dot_general | solution.py:59
  128.0 0.2 copy.34
  128.2 28.9 %all_to_all.16 = bf16[4,256,1024]{2,1,0:T(8,128)(2,1)} all-to-all(bf16[4,256,1024]{2,1,0:T(8,128)(2,1)S(1)} %bitcast.41), channel_id=1, replica_groups=mesh['seq'=32,'sub'=4] {'sub'}, dimensions={0} | all-to-all | bytes 4194304 | tf_op jit(solution)/shard_map/all_to_all | solution.py:15
  157.1 2.9 %reduce_sum.54 = bf16[256,1024]{1,0:T(8,128)(2,1)} reduce(bf16[4,256,1024]{2,1,0:T(8,128)(2,1)} %all_to_all.16, bf16[]{:T(256)} %constant.25.clone.1), dimensions={0}, to_apply=%region_6.7 | reduce | flops 786432 | bytes 2621442 | tf_op jit(solution)/shard_map/reduce_sum | solution.py:16
  (16 shorter events, 0.2 us)
Async XLA Ops:
  0.0 3.4 %copy-start = (bf16[256,4096]{1,0:T(8,128)(2,1)S(1)}, bf16[256,4096]{1,0:T(8,128)(2,1)}, u32[]{:S(2)}) copy-start(bf16[256,4096]{1,0:T(8,128)(2,1)} %param.8) | copy-start | bytes 6291460
  59.6 5.8 %copy-start.2 = (bf16[1,1024,1024]{2,1,0:T(8,128)(2,1)S(1)}, bf16[1,1024,1024]{2,1,0:T(8,128)(2,1)}, u32[]{:S(2)}) copy-start(bf16[1,1024,1024]{2,1,0:T(8,128)(2,1)} %param.12) | copy-start | bytes 6291460
  72.1 6.1 %copy-start.1 = (s32[1,256,2]{1,2,0:T(2,128)S(1)}, s32[1,256,2]{1,2,0:T(2,128)}, u32[]{:S(2)}) copy-start(s32[1,256,2]{1,2,0:T(2,128)} %param.14) | copy-start | bytes 6148
  72.1 35.4 %all-to-all-start.1 = ((bf16[128,6,1024]{2,1,0:T(8,128)(2,1)}), bf16[128,6,1024]{2,1,0:T(8,128)(2,1)}, u32[]{:S(2)}, u32[]{:S(2)}) async-start(bf16[128,6,1024]{2,1,0:T(8,128)(2,1)} %reshape.111), calls=%async_computation.1 | async-start | bytes 4194304 | tf_op jit(solution)/shard_map/all_to_all | solution.py:51
where the time goes:
time: 161 us; the launch traced here: 160 us
  blocking collectives  70.5 us (44%)
  waiting for transfers between devices  29.1 us (18%)
  local copies, waits for them, and re-layouts  23.9 us (15%)
  matrix products  21.8 us (14%)
  other arithmetic  8.83 us (5%)
  starting transfers between devices  5.72 us (4%)
    all_to_all x1, blocking collectives, body(): lax.all_to_all(packed, ('seq', 'sub'), split_axis=0, concat_axis=0, tiled...  41.5 us
    all_to_all x1, waiting for transfers between devices, body(): lax.all_to_all(answered, ('seq', 'sub'), split_axis=0, concat_axis=0, til...  29.1 us
    all_to_all x1, blocking collectives, summed_on_arrival(): lax.all_to_all(blocks, axis, split_axis=0, concat_axis=0, tiled=True)  28.9 us
    dot_general x1, matrix products, body(): jnp.dot(chosen, sub_tok, preferred_element_type=jnp.float32)  7.27 us
    dot_general x1, matrix products, expert_rows(): jnp.dot(rows_flat, expert_in[0], preferred_element_type=jnp.float32)  5.8 us
    dot_general x1, matrix products, body(): jnp.dot(head_out, w_merge, preferred_element_type=jnp.float32)  5.72 us
    all_to_all x1, starting transfers between devices, body(): lax.all_to_all(answered, ('seq', 'sub'), split_axis=0, concat_axis=0, til...  5.72 us
    gather x1, local copies, waits for them, and re-layouts, body(): gathered = returned_rows[jnp.maximum(slot_index, 0)].astype(jnp.float32)  4.34 us
  transfers between devices with their start and end apart: 1, of which 1 were waited for; matrix products, arithmetic and copies ran while one was open for 0% of the time, Pallas kernels for 0%

commit v1 on v0

v1 whole, which is shorter than its diff:
```python
import jax
import jax.numpy as jnp
from jax import lax
from jax.experimental import pallas as pl
from jax.experimental.pallas import tpu as pltpu
from jax.sharding import PartitionSpec as P

MESH = pl.DeviceIdType.MESH
PEERS = 128
MUL = 45
INV = 37
PARTS = 4
PER = PEERS // PARTS
SLOTS = 6
PAD = 8


def my_coords():
    s = lax.axis_index("seq")
    u = lax.axis_index("sub")
    return s % 4, s // 8, ((s // 4) % 2) * 2 + u // 2, u % 2


def device_at(x, y, z, c):
    return (y * 8 + (z // 2) * 4 + x, (z % 2) * 2 + c)


def peer(me, i, sign):
    r = (i * MUL) % PEERS
    dc = r % 2
    dx = (r // 2) % 4
    dz = (r // 8) % 4
    dy = r // 32
    x, y, z, c = me
    if sign < 0:
        dx, dz, dy = 4 - dx, 4 - dz, 4 - dy
    return device_at((x + dx) % 4, (y + dy) % 4, (z + dz) % 4, (c + dc) % 2)


def dot(a, b):
    return jnp.dot(a, b, preferred_element_type=jnp.float32)


def kernel(
    ids, quota, cap, tokens_h, ws_h, wm_h, win_h, wout_h,
    out,
    tokens, ws, wm, win, wout, sub_tok, chosen, comb, packed, recv, act, ans, ret, head, headb,
    dd_s, dd_r, z_s, z_r, f_s, f_r, keep,
    ld_sem, wm_sem, ds_sem, dr_sem, rs_sem, rr_sem, dd_ss, dd_rs, z_ss, z_rs, f_ss, f_rs,
):
    me = my_coords()
    mx, my, mz, mc = me
    zl = mz % 2
    barrier = pltpu.get_barrier_semaphore()

    loads = [pltpu.make_async_copy(tokens_h, tokens, ld_sem.at[0])]
    for n in range(4):
        loads.append(pltpu.make_async_copy(ws_h.at[:, pl.ds(n * 256, 256)], ws.at[n], ld_sem.at[1 + n]))
    loads.append(pltpu.make_async_copy(win_h, win, ld_sem.at[5]))
    loads.append(pltpu.make_async_copy(wout_h, wout, ld_sem.at[6]))
    quarters = [
        (1 - zl) * 2 + (1 - mc),
        (1 - zl) * 2 + mc,
        zl * 2 + (1 - mc),
        zl * 2 + mc,
    ]
    for n in range(4):
        col = pl.multiple_of(quarters[n] * 1024, 1024)
        loads.append(pltpu.make_async_copy(wm_h.at[:, pl.ds(col, 1024)], wm.at[n], wm_sem.at[n]))
    for cp in loads:
        cp.start()

    def clear(i, carry):
        ret[pl.ds(i * 8, 8)] = jnp.zeros((8, PAD, 1024), jnp.bfloat16)
        return carry

    lax.fori_loop(0, 16, clear, 0)

    def greet(i, carry):
        pl.semaphore_signal(barrier, inc=1, device_id=peer(me, i, 1), device_id_type=MESH)
        return carry

    lax.fori_loop(1, PEERS, greet, 0)

    e = lax.broadcasted_iota(jnp.int32, (128, 256), 0)
    id0 = ids[0:1, :]
    id1 = ids[1:2, :]
    oh0 = (e == id0).astype(jnp.float32)
    oh1 = (e == id1).astype(jnp.float32)
    tri = (
        lax.broadcasted_iota(jnp.int32, (256, 256), 0) < lax.broadcasted_iota(jnp.int32, (256, 256), 1)
    ).astype(jnp.bfloat16)
    before = dot((oh0 + oh1).astype(jnp.bfloat16), tri)
    rank0 = jnp.sum(oh0 * before, axis=0, keepdims=True)
    rank1 = jnp.sum(oh1 * before, axis=0, keepdims=True)
    sq0 = lax.broadcasted_iota(jnp.int32, (128, 128), 0)
    sq1 = lax.broadcasted_iota(jnp.int32, (128, 128), 1)
    cap_col = jnp.sum(jnp.where(sq0 == sq1, cap[0:1, :].astype(jnp.float32), 0.0), axis=1, keepdims=True)
    lim0 = jnp.sum(oh0 * cap_col, axis=0, keepdims=True)
    lim1 = jnp.sum(oh1 * cap_col, axis=0, keepdims=True)

    def place(ident):
        ec = ident & 1
        ex = (ident >> 2) & 3
        ez = ((ident >> 4) & 1) * 2 + ((ident >> 1) & 1)
        ey = ident >> 5
        r = (((ey - my) & 3) << 5) + (((ez - mz) & 3) << 3) + (((ex - mx) & 3) << 1) + ((ec - mc) & 1)
        return ((r * INV) & (PEERS - 1)) * PAD

    loc0 = place(id0) + rank0.astype(jnp.int32)
    loc1 = place(id1) + rank1.astype(jnp.int32)
    w0 = jnp.where(rank0 < lim0, quota[0:1, :].astype(jnp.float32) * (1.0 / 65536.0), 0.0)
    w1 = jnp.where(rank1 < lim1, quota[1:2, :].astype(jnp.float32) * (1.0 / 65536.0), 0.0)

    for j in range(4):
        p = lax.broadcasted_iota(jnp.int32, (256, 256), 0) + j * 256
        hit = jnp.logical_or(p == loc0, p == loc1)
        chosen[pl.ds(j * 256, 256)] = jnp.where(hit, 1.0, 0.0).astype(jnp.bfloat16)
    rows = jnp.concatenate(
        [loc0.astype(jnp.float32), loc1.astype(jnp.float32), w0, w1, jnp.zeros((4, 256), jnp.float32)], axis=0
    )
    cols = rows.T
    l0 = cols[:, 0:1]
    l1 = cols[:, 1:2]
    v0 = cols[:, 2:3]
    v1 = cols[:, 3:4]
    for j in range(4):
        p = (lax.broadcasted_iota(jnp.int32, (256, 256), 1) + j * 256).astype(jnp.float32)
        c = jnp.where(p == l0, v0, jnp.where(p == l1, v1, 0.0))
        comb[j] = c.astype(jnp.bfloat16)

    loads[0].wait()
    for n in range(4):
        loads[1 + n].wait()
        sub_tok[:, pl.ds(n * 256, 256)] = dot(tokens[...], ws[n]).astype(jnp.bfloat16)

    for j in range(PARTS):
        rows_j = dot(chosen[pl.ds(j * 256, 256)], sub_tok[...]).astype(jnp.bfloat16)
        packed[pl.ds(j * PER, PER)] = rows_j.reshape(PER, PAD, 1024)

    pl.semaphore_wait(barrier, PEERS - 1)

    def six(ref, i):
        return ref.at[i, pl.ds(0, SLOTS)]

    def six_many(ref, i, n):
        return ref.at[pl.ds(i, n), pl.ds(0, SLOTS)]

    def dispatch(i, carry):
        pltpu.make_async_remote_copy(
            src_ref=six(packed, i), dst_ref=six(recv, i),
            send_sem=ds_sem, recv_sem=dr_sem.at[i // PER],
            device_id=peer(me, i, 1), device_id_type=MESH,
        ).start()
        return carry

    lax.fori_loop(1, PEERS, dispatch, 0)
    recv[0] = packed[0]

    loads[5].wait()
    loads[6].wait()

    def landed(ref, sem, j):
        if j == 0:
            return pltpu.make_async_copy(six_many(ref, 1, PER - 1), six_many(ref, 1, PER - 1), sem.at[0])
        return pltpu.make_async_copy(six_many(ref, j * PER, PER), six_many(ref, j * PER, PER), sem.at[j])

    for j in range(PARTS):
        landed(recv, dr_sem, j).wait()
        x = recv[pl.ds(j * PER, PER)].reshape(PER * PAD, 1024)
        for n in range(4):
            g = dot(x, win[:, pl.ds(n * 256, 256)])
            u = dot(x, win[:, pl.ds(1024 + n * 256, 256)])
            act[:, pl.ds(n * 256, 256)] = (g / (1.0 + jnp.exp(-g)) * u).astype(jnp.bfloat16)
        for n in range(4):
            r = dot(act[...], wout[:, pl.ds(n * 256, 256)]).astype(jnp.bfloat16)
            ans[pl.ds(j * PER, PER), :, pl.ds(n * 256, 256)] = r.reshape(PER, PAD, 256)

        def give_back(i, carry):
            pltpu.make_async_remote_copy(
                src_ref=six(ans, i), dst_ref=six(ret, i),
                send_sem=rs_sem, recv_sem=rr_sem.at[j],
                device_id=peer(me, i, -1), device_id_type=MESH,
            ).start()
            return carry

        lax.fori_loop(max(1, j * PER), (j + 1) * PER, give_back, 0)
        if j == 0:
            ret[0] = ans[0]

    for j in range(PARTS):
        landed(ret, rr_sem, j).wait()
        part = dot(comb[j], ret[pl.ds(j * PER, PER)].reshape(PER * PAD, 1024))
        if j == 0:
            head[...] = part
        elif j < PARTS - 1:
            head[...] += part
        else:
            headb[...] = (head[...] + part).astype(jnp.bfloat16)

    for n in range(4):
        loads[7 + n].wait()

    partner = device_at(mx, my, mz, 1 - mc)
    across = device_at(mx, my, mz + 1 - 2 * zl, mc)

    def send(src, dst, ss, rs, b, to):
        return pltpu.make_async_remote_copy(
            src_ref=src.at[b], dst_ref=dst.at[b], send_sem=ss.at[b], recv_sem=rs.at[b],
            device_id=to, device_id_type=MESH,
        )

    def product(n, b):
        return dot(headb[...], wm[n, :, pl.ds(b * 256, 256)])

    def first(b):
        dd_s[b] = product(0, b).astype(jnp.bfloat16)
        send(dd_s, dd_r, dd_ss, dd_rs, b, partner).start()

    def second(b):
        mine = product(1, b)
        send(dd_s, dd_r, dd_ss, dd_rs, b, partner).wait_recv()
        z_s[b] = (mine + dd_r[b].astype(jnp.float32)).astype(jnp.bfloat16)
        send(z_s, z_r, z_ss, z_rs, b, across).start()

    first(0)
    first(1)
    second(0)
    first(2)
    second(1)
    first(3)
    second(2)
    second(3)
    for b in range(4):
        f_s[b] = product(2, b).astype(jnp.bfloat16)
        send(f_s, f_r, f_ss, f_rs, b, partner).start()
    for b in range(4):
        keep[b] = product(3, b)
    for b in range(4):
        send(f_s, f_r, f_ss, f_rs, b, partner).wait_recv()
        keep[b] += f_r[b].astype(jnp.float32)
    for b in range(4):
        send(z_s, z_r, z_ss, z_rs, b, across).wait_recv()
        out[:, pl.ds(b * 256, 256)] = (keep[b] + z_r[b].astype(jnp.float32)).astype(jnp.bfloat16)

    pltpu.make_async_copy(six_many(packed, 1, PEERS - 1), six_many(packed, 1, PEERS - 1), ds_sem).wait()
    pltpu.make_async_copy(six_many(ans, 1, PEERS - 1), six_many(ans, 1, PEERS - 1), rs_sem).wait()
    for b in range(4):
        send(dd_s, dd_r, dd_ss, dd_rs, b, partner).wait_send()
        send(z_s, z_r, z_ss, z_rs, b, across).wait_send()
        send(f_s, f_r, f_ss, f_rs, b, partner).wait_send()


def body(tokens, w_split, w_merge, expert_in, expert_out, expert_ids, combine_q, capacity):
    bf, f32 = jnp.bfloat16, jnp.float32
    vmem = pl.BlockSpec(memory_space=pltpu.VMEM)
    hbm = pl.BlockSpec(memory_space=pl.ANY)
    dma = pltpu.SemaphoreType.DMA
    quarter = pltpu.VMEM((4, 256, 256), bf)
    return pl.pallas_call(
        kernel,
        out_shape=jax.ShapeDtypeStruct((256, 1024), bf),
        in_specs=[vmem] * 3 + [hbm] * 5,
        out_specs=vmem,
        scratch_shapes=[
            pltpu.VMEM((256, 4096), bf),
            pltpu.VMEM((4, 4096, 256), bf),
            pltpu.VMEM((4, 1024, 1024), bf),
            pltpu.VMEM((1024, 2048), bf),
            pltpu.VMEM((1024, 1024), bf),
            pltpu.VMEM((256, 1024), bf),
            pltpu.VMEM((1024, 256), bf),
            pltpu.VMEM((4, 256, 256), bf),
            pltpu.VMEM((PEERS, PAD, 1024), bf),
            pltpu.VMEM((PEERS, PAD, 1024), bf),
            pltpu.VMEM((PER * PAD, 1024), bf),
            pltpu.VMEM((PEERS, PAD, 1024), bf),
            pltpu.VMEM((PEERS, PAD, 1024), bf),
            pltpu.VMEM((256, 1024), f32),
            pltpu.VMEM((256, 1024), bf),
            quarter, quarter, quarter, quarter, quarter, quarter,
            pltpu.VMEM((4, 256, 256), f32),
            dma((7,)), dma((4,)), dma, dma((PARTS,)), dma, dma((PARTS,)),
            dma((4,)), dma((4,)), dma((4,)), dma((4,)), dma((4,)), dma((4,)),
        ],
        compiler_params=pltpu.CompilerParams(
            collective_id=0, has_side_effects=True, vmem_limit_bytes=58 * 2**20
        ),
    )(
        expert_ids[0].T,
        combine_q[0].T,
        capacity.reshape(1, -1),
        tokens,
        w_split,
        w_merge,
        expert_in[0],
        expert_out[0],
    )


def solution(mesh):
    in_specs = (
        P("seq", None),
        P(None, "sub"),
        P("sub", None),
        P(("seq", "sub"), None, None),
        P(("seq", "sub"), None, None),
        P("sub", "seq", None),
        P("sub", "seq", None),
        P(),
    )
    return jax.shard_map(body, mesh=mesh, in_specs=in_specs, out_specs=P("seq", "sub"), check_vma=False)
```

time: 161 us -> 76.3 us (0.47)
  Pallas kernels: 0 us -> 74.3 us
  blocking collectives: 70.5 us -> 0 us
  waiting for transfers between devices: 29.1 us -> 0 us
  local copies, waits for them, and re-layouts: 23.9 us -> 1.87 us
  matrix products: 21.8 us -> 0 us
  other arithmetic: 8.83 us -> 0 us
  starting transfers between devices: 5.72 us -> 0 us
    pallas_call x0 -> x1, Pallas kernels: none -> 74.3 us  [body(): pl.pallas_call(kernel, out_shape=jax.ShapeDtypeStruct((256, 1024), bf), i...]
    all_to_all x2 -> x0, blocking collectives: 70.5 us -> none  [the longest x1 41.5 us: body(): lax.all_to_all(packed, ('seq', 'sub'), split_axis=0, concat_axis=0, tiled...]
    all_to_all x1 -> x0, waiting for transfers between devices: 29.1 us -> none  [body(): lax.all_to_all(answered, ('seq', 'sub'), split_axis=0, concat_axis=0, til...]
    dot_general x4 -> x0, matrix products: 21.8 us -> none  [the longest x1 7.27 us: body(): jnp.dot(chosen, sub_tok, preferred_element_type=jnp.float32)]
    reshape x5 -> x0, local copies, waits for them, and re-layouts: 15 us -> none  [the longest x1 3.73 us: expert_rows(): rows_flat = received.reshape(-1, dims_in[-1])]
    reduce_sum x3 -> x0, other arithmetic: 8.21 us -> none  [the longest x1 4.33 us: body(): head_out = jnp.sum(weighted, axis=1).astype(jnp.bfloat16)]
    all_to_all x1 -> x0, starting transfers between devices: 5.72 us -> none  [body(): lax.all_to_all(answered, ('seq', 'sub'), split_axis=0, concat_axis=0, til...]
    gather x1 -> x0, local copies, waits for them, and re-layouts: 4.34 us -> none  [body(): gathered = returned_rows[jnp.maximum(slot_index, 0)].astype(jnp.float32)]
  transfers between devices with their start and end apart: 1 -> 0, of which waited for: 1 -> 0; matrix products, arithmetic and copies ran while one was open for 0% -> 0% of each run, Pallas kernels for 0% -> 0%
where the time goes in v1:
time: 76.3 us; the launch traced here: 76.1 us
  Pallas kernels  74.3 us (97%)
  local copies, waits for them, and re-layouts  1.87 us (2%)
    pallas_call x1, Pallas kernels, body(): pl.pallas_call(kernel, out_shape=jax.ShapeDtypeStruct((256, 1024), bf), i...  74.3 us
    unnamed x1, local copies, waits for them, and re-layouts  1.87 us

profile of v1, /device:TPU:1, one launch (start us, length us, event | category | flops | bytes accessed | tf_op | source)
XLA Modules:
  0.0 76.1 jit_solution(10344112434387445526)
XLA Ops:
  0.0 74.3 %shard_map.82 = bf16[256,1024]{1,0:T(8,128)(2,1)} custom-call(s32[2,256]{1,0:T(2,128)} %bitcast.11, s32[2,256]{1,0:T(2,128)} %bitcast.12, s32[1,128]{1,0:T(1,128)} %bitcast.13, bf16[256,4096]{1,0:T(8,128)(2,1)} %tokens_h.1, bf16[4096,1024]{1,0:T(8,128)(2,1)} %ws_h.1, bf16[1024,4096]{1,0:T(8,128)(2,1)} %wm_h.1, bf16[1024,2048]{1,0:T(8,128)(2,1)} %bitcast.9, ...), custom_call_target="tpu_custom_call" | custom-call | tf_op jit(solution)/shard_map/pallas_call | solution.py:260
  74.3 1.9 %copy.10 = bf16[256,1024]{1,0:T(8,128)(2,1)} copy(bf16[256,1024]{1,0:T(8,128)(2,1)} %shard_map.82) | data formatting | bytes 1048576

commit v2 on v0

v2 whole, which is shorter than its diff:
```python
import jax
import jax.numpy as jnp
import numpy as np
from jax import lax
from jax.experimental import pallas as pl
from jax.experimental.pallas import tpu as pltpu
from jax.sharding import PartitionSpec as P

MESH = pl.DeviceIdType.MESH
PEERS = 128
SLOTS = 6
PAD = 8
EDGES = (0, 32, 64, 96, 128)
EARLY = 40
MUL = 45
PARTS = len(EDGES) - 1


def step_of(r):
    return (r // 2) % 4, r // 32, (r // 8) % 4, r % 2


def hops(r):
    return sum((0, 1, 2, 1)[d] for d in step_of(r)[:3])


def mixed():
    return [(i * MUL) % PEERS for i in range(1, PEERS)] + [0]


ORDER = mixed()
POSITION = np.argsort(np.array(ORDER)).astype(np.int32)


def part_of(i):
    return max(j for j in range(PARTS) if EDGES[j] <= i)


def dot(a, b):
    return jnp.dot(a, b, preferred_element_type=jnp.float32)


def kernel(
    ids_h, quota_h, cap_h, table_h, tokens_h, ws_h, wm_h, win_h, wout_h,
    keep, z_r,
    ids, quota, cap, table,
    tokens, ws, wm, win, wout, sub_tok, chosen, comb, packed, recv, act, ans, ret, head, headb,
    dd_s, dd_r, z_s, f_s, f_r,
    sm_sem, ld_sem, wm_sem, ds_sem, dr_sem, rs_sem, rr_sem, dd_ss, dd_rs, z_ss, z_rs, f_ss, f_rs,
):
    s = lax.axis_index("seq")
    u = lax.axis_index("sub")
    mx, my, mz, mc = s % 4, s // 8, ((s // 4) % 2) * 2 + u // 2, u % 2
    zl = mz % 2
    xs = [(mx + d) % 4 for d in range(4)]
    ys = [((my + d) % 4) * 8 for d in range(4)]
    zs = [(mz + d) % 4 for d in range(4)]
    zh = [(z // 2) * 4 for z in zs]
    zw = [(z % 2) * 2 for z in zs]
    cs = [(mc + d) % 2 for d in range(2)]

    def peer(i, sign=1):
        dx, dy, dz, dc = step_of(ORDER[i])
        if sign < 0:
            dx, dy, dz = -dx % 4, -dy % 4, -dz % 4
        return (ys[dy] + zh[dz] + xs[dx], zw[dz] + cs[dc])

    barrier = pltpu.get_barrier_semaphore()

    loads = [pltpu.make_async_copy(tokens_h, tokens, ld_sem.at[0])]
    for n in range(2):
        loads.append(pltpu.make_async_copy(ws_h.at[:, pl.ds(n * 512, 512)], ws.at[n], ld_sem.at[1 + n]))
    small = [
        pltpu.make_async_copy(ids_h, ids, sm_sem.at[0]),
        pltpu.make_async_copy(quota_h, quota, sm_sem.at[1]),
        pltpu.make_async_copy(cap_h, cap, sm_sem.at[2]),
        pltpu.make_async_copy(table_h, table, sm_sem.at[3]),
    ]
    for cp in small + loads:
        cp.start()
    for i in sorted(range(PEERS - 1), key=lambda i: -hops(ORDER[i])):
        pl.semaphore_signal(barrier, inc=1, device_id=peer(i), device_id_type=MESH)

    loads.append(pltpu.make_async_copy(win_h, win, ld_sem.at[3]))
    loads.append(pltpu.make_async_copy(wout_h, wout, ld_sem.at[4]))
    quarters = [
        (1 - zl) * 2 + (1 - mc),
        (1 - zl) * 2 + mc,
        zl * 2 + (1 - mc),
        zl * 2 + mc,
    ]
    for n in range(4):
        col = pl.multiple_of(quarters[n] * 1024, 1024)
        loads.append(pltpu.make_async_copy(wm_h.at[:, pl.ds(col, 1024)], wm.at[n], wm_sem.at[n]))

    def clear(i, carry):
        ret[pl.ds(i * 8, 8)] = jnp.zeros((8, PAD, 1024), jnp.bfloat16)
        return carry

    lax.fori_loop(0, 16, clear, 0)

    with jax.named_scope("small"):
        for cp in small:
            cp.wait()
    with jax.named_scope("route"):
        e = lax.broadcasted_iota(jnp.int32, (128, 256), 0)
        id0 = ids[0:1, :]
        id1 = ids[1:2, :]
        oh0 = (e == id0).astype(jnp.float32)
        oh1 = (e == id1).astype(jnp.float32)
        tri = (
            lax.broadcasted_iota(jnp.int32, (256, 256), 0) < lax.broadcasted_iota(jnp.int32, (256, 256), 1)
        ).astype(jnp.bfloat16)
        before = dot((oh0 + oh1).astype(jnp.bfloat16), tri)
        rank0 = jnp.sum(oh0 * before, axis=0, keepdims=True)
        rank1 = jnp.sum(oh1 * before, axis=0, keepdims=True)
        sq0 = lax.broadcasted_iota(jnp.int32, (128, 128), 0)
        sq1 = lax.broadcasted_iota(jnp.int32, (128, 128), 1)
        cap_col = jnp.sum(jnp.where(sq0 == sq1, cap[0:1, :].astype(jnp.float32), 0.0), axis=1, keepdims=True)
        ec = sq0 & 1
        ex = (sq0 >> 2) & 3
        ez = ((sq0 >> 4) & 1) * 2 + ((sq0 >> 1) & 1)
        ey = sq0 >> 5
        r = (((ey - my) & 3) << 5) + (((ez - mz) & 3) << 3) + (((ex - mx) & 3) << 1) + ((ec - mc) & 1)
        pos_col = jnp.sum(jnp.where(r == sq1, table[0:1, :].astype(jnp.float32), 0.0), axis=1, keepdims=True)
        lim0 = jnp.sum(oh0 * cap_col, axis=0, keepdims=True)
        lim1 = jnp.sum(oh1 * cap_col, axis=0, keepdims=True)
        loc0 = jnp.sum(oh0 * pos_col, axis=0, keepdims=True) * PAD + rank0
        loc1 = jnp.sum(oh1 * pos_col, axis=0, keepdims=True) * PAD + rank1
        w0 = jnp.where(rank0 < lim0, quota[0:1, :].astype(jnp.float32) * (1.0 / 65536.0), 0.0)
        w1 = jnp.where(rank1 < lim1, quota[1:2, :].astype(jnp.float32) * (1.0 / 65536.0), 0.0)

        for j in range(4):
            p = (lax.broadcasted_iota(jnp.int32, (256, 256), 0) + j * 256).astype(jnp.float32)
            hit = jnp.logical_or(p == loc0, p == loc1)
            chosen[pl.ds(j * 256, 256)] = jnp.where(hit, 1.0, 0.0).astype(jnp.bfloat16)

    def six(ref, i, half):
        return ref.at[i, pl.ds(0, SLOTS), pl.ds(half * 512, 512)]

    def row(ref, i):
        return ref.at[i, pl.ds(0, SLOTS)]

    def rows(ref, i, n):
        return ref.at[pl.ds(i, n), pl.ds(0, SLOTS)]

    def out_to(src, dst, i):
        pltpu.make_async_remote_copy(
            src_ref=src, dst_ref=dst, send_sem=ds_sem, recv_sem=dr_sem.at[part_of(i)],
            device_id=peer(i), device_id_type=MESH,
        ).start()

    loads[0].wait()
    for half in range(2):
        with jax.named_scope(f"split{half}"):
            loads[1 + half].wait()
            cols = pl.ds(half * 512, 512)
            sub_tok[:, cols] = dot(tokens[...], ws[half]).astype(jnp.bfloat16)
        with jax.named_scope(f"pack{half}"):
            if half == 1:
                for cp in loads[3:]:
                    cp.start()
            for j in range(4):
                rows_j = dot(chosen[pl.ds(j * 256, 256)], sub_tok[:, cols]).astype(jnp.bfloat16)
                packed[pl.ds(j * 32, 32), :, cols] = rows_j.reshape(32, PAD, 512)
        with jax.named_scope(f"send{half}"):
            if half == 0:
                pl.semaphore_wait(barrier, PEERS - 1)
            for i in range(EARLY):
                out_to(six(packed, i, half), six(recv, i, half), i)
    with jax.named_scope("send_rest"):
        for i in range(EARLY, PEERS - 1):
            out_to(row(packed, i), row(recv, i), i)
    recv[PEERS - 1] = packed[PEERS - 1]

    with jax.named_scope("comb"):
        stacked = jnp.concatenate([loc0, loc1, w0, w1, jnp.zeros((4, 256), jnp.float32)], axis=0)
        turned = stacked.T
        l0 = turned[:, 0:1]
        l1 = turned[:, 1:2]
        v0 = turned[:, 2:3]
        v1 = turned[:, 3:4]
        for j in range(4):
            p = (lax.broadcasted_iota(jnp.int32, (256, 256), 1) + j * 256).astype(jnp.float32)
            c = jnp.where(p == l0, v0, jnp.where(p == l1, v1, 0.0))
            comb[:, pl.ds(j * 256, 256)] = c.astype(jnp.bfloat16)

    loads[3].wait()
    loads[4].wait()

    def landed(ref, sem, j):
        lo, hi = EDGES[j], min(EDGES[j + 1], PEERS - 1)
        return pltpu.make_async_copy(rows(ref, lo, hi - lo), rows(ref, lo, hi - lo), sem.at[j])

    def give_back(j):
        with jax.named_scope(f"back{j}"):
            for i in range(EDGES[j], min(EDGES[j + 1], PEERS - 1)):
                pltpu.make_async_remote_copy(
                    src_ref=row(ans, i), dst_ref=row(ret, i),
                    send_sem=rs_sem, recv_sem=rr_sem.at[j],
                    device_id=peer(i, -1), device_id_type=MESH,
                ).start()

    for j in range(PARTS):
        lo, n_rows = EDGES[j], (EDGES[j + 1] - EDGES[j]) * PAD
        with jax.named_scope(f"wait{j}"):
            landed(recv, dr_sem, j).wait()
        with jax.named_scope(f"ffn{j}"):
            x = recv[pl.ds(lo, n_rows // PAD)].reshape(n_rows, 1024)
            for n in range(4):
                g = dot(x, win[:, pl.ds(n * 256, 256)])
                t = dot(x, win[:, pl.ds(1024 + n * 256, 256)])
                act[pl.ds(0, n_rows), pl.ds(n * 256, 256)] = (g / (1.0 + jnp.exp(-g)) * t).astype(jnp.bfloat16)
            for n in range(2):
                a = dot(act[pl.ds(0, n_rows)], wout[:, pl.ds(n * 512, 512)]).astype(jnp.bfloat16)
                ans[pl.ds(lo, n_rows // PAD), :, pl.ds(n * 512, 512)] = a.reshape(n_rows // PAD, PAD, 512)
        give_back(j)
    ret[PEERS - 1] = ans[PEERS - 1]

    for n in range(4):
        loads[5 + n].wait()
    for j in range(PARTS):
        lo, n_rows = EDGES[j], (EDGES[j + 1] - EDGES[j]) * PAD
        with jax.named_scope(f"rwait{j}"):
            landed(ret, rr_sem, j).wait()
        part = dot(comb[:, pl.ds(lo * PAD, n_rows)], ret[pl.ds(lo, n_rows // PAD)].reshape(n_rows, 1024))
        if j == 0:
            head[...] = part
        elif j < PARTS - 1:
            head[...] += part
        else:
            headb[...] = (head[...] + part).astype(jnp.bfloat16)

    partner = (ys[0] + zh[0] + xs[0], zw[0] + cs[1])
    across = (ys[0] + zh[0] + xs[0], (2 - zw[0]) + cs[0])

    def send(src, dst, ss, rs, b, to):
        return pltpu.make_async_remote_copy(
            src_ref=src.at[b], dst_ref=dst.at[b], send_sem=ss.at[b], recv_sem=rs.at[b],
            device_id=to, device_id_type=MESH,
        )

    def send_z(b):
        return pltpu.make_async_remote_copy(
            src_ref=z_s.at[b], dst_ref=z_r.at[:, pl.ds(b * 256, 256)], send_sem=z_ss.at[b], recv_sem=z_rs.at[b],
            device_id=across, device_id_type=MESH,
        )

    def product(n, b, width=256):
        return dot(headb[...], wm[n, :, pl.ds(b * 256, width)])

    def first(b):
        dd_s[b] = product(0, b).astype(jnp.bfloat16)
        send(dd_s, dd_r, dd_ss, dd_rs, b, partner).start()

    def second(b):
        mine = product(1, b)
        send(dd_s, dd_r, dd_ss, dd_rs, b, partner).wait_recv()
        z_s[b] = (mine + dd_r[b].astype(jnp.float32)).astype(jnp.bfloat16)
        send_z(b).start()

    with jax.named_scope("merge"):
        first(0)
        first(1)
        second(0)
        first(2)
        second(1)
        first(3)
        second(2)
        second(3)
    with jax.named_scope("merge_near"):
        for b in range(4):
            f_s[b] = product(2, b).astype(jnp.bfloat16)
            send(f_s, f_r, f_ss, f_rs, b, partner).start()
        for b in range(2):
            keep[:, pl.ds(b * 512, 512)] = product(3, 2 * b, 512)
        for b in range(4):
            send(f_s, f_r, f_ss, f_rs, b, partner).wait_recv()
            keep[:, pl.ds(b * 256, 256)] += f_r[b].astype(jnp.float32)
        pltpu.make_async_copy(rows(packed, 0, PEERS - 1), rows(packed, 0, PEERS - 1), ds_sem).wait()
        pltpu.make_async_copy(rows(ans, 0, PEERS - 1), rows(ans, 0, PEERS - 1), rs_sem).wait()
        for b in range(4):
            send(dd_s, dd_r, dd_ss, dd_rs, b, partner).wait_send()
            send(f_s, f_r, f_ss, f_rs, b, partner).wait_send()
    with jax.named_scope("final"):
        for b in range(4):
            send_z(b).wait_send()
        for b in range(4):
            send_z(b).wait_recv()


def body(tokens, w_split, w_merge, expert_in, expert_out, expert_ids, combine_q, capacity):
    bf, f32, i32 = jnp.bfloat16, jnp.float32, jnp.int32
    hbm = pl.BlockSpec(memory_space=pl.ANY)
    vm = pl.BlockSpec(memory_space=pltpu.VMEM)
    dma = pltpu.SemaphoreType.DMA
    quarter = pltpu.VMEM((4, 256, 256), bf)
    slots = pltpu.VMEM((PEERS, PAD, 1024), bf)
    mine, other = pl.pallas_call(
        kernel,
        out_shape=[pltpu.VMEM((256, 1024), f32), pltpu.VMEM((256, 1024), bf)],
        in_specs=[hbm] * 9,
        out_specs=[vm, vm],
        scratch_shapes=[
            pltpu.VMEM((2, 256), i32),
            pltpu.VMEM((2, 256), i32),
            pltpu.VMEM((1, 128), i32),
            pltpu.VMEM((1, 128), i32),
            pltpu.VMEM((256, 4096), bf),
            pltpu.VMEM((2, 4096, 512), bf),
            pltpu.VMEM((4, 1024, 1024), bf),
            pltpu.VMEM((1024, 2048), bf),
            pltpu.VMEM((1024, 1024), bf),
            pltpu.VMEM((256, 1024), bf),
            pltpu.VMEM((1024, 256), bf),
            pltpu.VMEM((256, 1024), bf),
            slots,
            slots,
            pltpu.VMEM((max(b - a for a, b in zip(EDGES, EDGES[1:])) * PAD, 1024), bf),
            slots,
            slots,
            pltpu.VMEM((256, 1024), f32),
            pltpu.VMEM((256, 1024), bf),
            quarter, quarter, quarter, quarter, quarter,
            dma((4,)), dma((5,)), dma((4,)), dma, dma((PARTS,)), dma, dma((PARTS,)),
            dma((4,)), dma((4,)), dma((4,)), dma((4,)), dma((4,)), dma((4,)),
        ],
        compiler_params=pltpu.CompilerParams(
            collective_id=0, has_side_effects=True, vmem_limit_bytes=58 * 2**20
        ),
    )(
        expert_ids[0].T,
        combine_q[0].T,
        capacity.reshape(1, -1),
        jnp.asarray(POSITION).reshape(1, -1),
        tokens,
        w_split,
        w_merge,
        expert_in[0],
        expert_out[0],
    )
    return (mine + other.astype(f32)).astype(bf)


def solution(mesh):
    in_specs = (
        P("seq", None),
        P(None, "sub"),
        P("sub", None),
        P(("seq", "sub"), None, None),
        P(("seq", "sub"), None, None),
        P("sub", "seq", None),
        P("sub", "seq", None),
        P(),
    )
    return jax.shard_map(body, mesh=mesh, in_specs=in_specs, out_specs=P("seq", "sub"), check_vma=False)
```

time: 161 us -> 64.8 us (0.40)
  blocking collectives: 70.5 us -> 0 us
  Pallas kernels: 0 us -> 63.8 us
  waiting for transfers between devices: 29.1 us -> 0 us
  local copies, waits for them, and re-layouts: 23.9 us -> 0 us
  matrix products: 21.8 us -> 0 us
  other arithmetic: 8.83 us -> 0.94 us
  starting transfers between devices: 5.72 us -> 0 us
    all_to_all x2 -> x0, blocking collectives: 70.5 us -> none  [the longest x1 41.5 us: body(): lax.all_to_all(packed, ('seq', 'sub'), split_axis=0, concat_axis=0, tiled...]
    pallas_call x0 -> x1, Pallas kernels: none -> 63.8 us  [body(): pl.pallas_call(kernel, out_shape=[pltpu.VMEM((256, 1024), f32), pltpu.VME...]
    all_to_all x1 -> x0, waiting for transfers between devices: 29.1 us -> none  [body(): lax.all_to_all(answered, ('seq', 'sub'), split_axis=0, concat_axis=0, til...]
    dot_general x4 -> x0, matrix products: 21.8 us -> none  [the longest x1 7.27 us: body(): jnp.dot(chosen, sub_tok, preferred_element_type=jnp.float32)]
    reshape x5 -> x0, local copies, waits for them, and re-layouts: 15 us -> none  [the longest x1 3.73 us: expert_rows(): rows_flat = received.reshape(-1, dims_in[-1])]
    reduce_sum x3 -> x0, other arithmetic: 8.21 us -> none  [the longest x1 4.33 us: body(): head_out = jnp.sum(weighted, axis=1).astype(jnp.bfloat16)]
    all_to_all x1 -> x0, starting transfers between devices: 5.72 us -> none  [body(): lax.all_to_all(answered, ('seq', 'sub'), split_axis=0, concat_axis=0, til...]
    gather x1 -> x0, local copies, waits for them, and re-layouts: 4.34 us -> none  [body(): gathered = returned_rows[jnp.maximum(slot_index, 0)].astype(jnp.float32)]
  transfers between devices with their start and end apart: 1 -> 0, of which waited for: 1 -> 0; matrix products, arithmetic and copies ran while one was open for 0% -> 0% of each run, Pallas kernels for 0% -> 0%
where the time goes in v2:
time: 64.8 us; the launch traced here: 64.7 us
  Pallas kernels  63.8 us (98%)
  other arithmetic  0.94 us (1%)
    pallas_call x1, Pallas kernels, body(): pl.pallas_call(kernel, out_shape=[pltpu.VMEM((256, 1024), f32), pltpu.VME...  63.8 us

profile of v2, /device:TPU:1, one launch (start us, length us, event | category | flops | bytes accessed | tf_op | source)
XLA Modules:
  0.0 64.7 jit_solution(5133486930481498968)
XLA Ops:
  0.0 63.8 %shard_map.91 = (f32[256,1024]{1,0:T(8,128)S(1)}, bf16[256,1024]{1,0:T(8,128)(2,1)S(1)}) custom-call(s32[2,256]{1,0:T(2,128)} %bitcast.11, s32[2,256]{1,0:T(2,128)} %bitcast.12, s32[1,128]{1,0:T(1,128)} %bitcast.13, s32[1,128]{1,0:T(1,128)} %constant.7.table_h, bf16[256,4096]{1,0:T(8,128)(2,1)} %tokens_h.1, bf16[4096,1024]{1,0:T(8,128)(2,1)} %ws_h.1, ...), custom_call_target="tpu_custom_call" | custom-call | tf_op jit(solution)/shard_map/pallas_call | solution.py:299
  63.8 0.9 %add_convert_fusion = bf16[256,1024]{1,0:T(8,128)(2,1)} fusion(f32[256,1024]{1,0:T(8,128)S(1)} %get-tuple-element.7, bf16[256,1024]{1,0:T(8,128)(2,1)S(1)} %get-tuple-element.8), kind=kLoop, calls=%fused_computation | loop fusion | flops 786432 | bytes 2097152 | tf_op jit(solution)/shard_map/convert_element_type | solution.py:342

commit v3 on v2

--- a/solution.py
+++ b/solution.py
@@ -13,6 +13,7 @@
 EDGES = (0, 32, 64, 96, 128)
 EARLY = 40
 MUL = 45
+BLOCKS = ((0, 128), (128, 128), (256, 256), (512, 256), (768, 256))
 PARTS = len(EDGES) - 1
 
 
@@ -68,21 +69,25 @@
     barrier = pltpu.get_barrier_semaphore()
 
     loads = [pltpu.make_async_copy(tokens_h, tokens, ld_sem.at[0])]
-    for n in range(2):
-        loads.append(pltpu.make_async_copy(ws_h.at[:, pl.ds(n * 512, 512)], ws.at[n], ld_sem.at[1 + n]))
+    for n in range(4):
+        loads.append(pltpu.make_async_copy(ws_h.at[:, pl.ds(n * 256, 256)], ws.at[n], ld_sem.at[1 + n]))
     small = [
         pltpu.make_async_copy(ids_h, ids, sm_sem.at[0]),
         pltpu.make_async_copy(quota_h, quota, sm_sem.at[1]),
         pltpu.make_async_copy(cap_h, cap, sm_sem.at[2]),
         pltpu.make_async_copy(table_h, table, sm_sem.at[3]),
     ]
-    for cp in small + loads:
+    for cp in small:
         cp.start()
-    for i in sorted(range(PEERS - 1), key=lambda i: -hops(ORDER[i])):
+    greets = sorted(range(PEERS - 1), key=lambda i: -hops(ORDER[i]))
+    for k, i in enumerate(greets):
+        if k == 40:
+            for cp in loads[:3]:
+                cp.start()
         pl.semaphore_signal(barrier, inc=1, device_id=peer(i), device_id_type=MESH)
 
-    loads.append(pltpu.make_async_copy(win_h, win, ld_sem.at[3]))
-    loads.append(pltpu.make_async_copy(wout_h, wout, ld_sem.at[4]))
+    loads.append(pltpu.make_async_copy(win_h, win, ld_sem.at[5]))
+    loads.append(pltpu.make_async_copy(wout_h, wout, ld_sem.at[6]))
     quarters = [
         (1 - zl) * 2 + (1 - mc),
         (1 - zl) * 2 + mc,
@@ -152,14 +157,20 @@
 
     loads[0].wait()
     for half in range(2):
+        cols = pl.ds(half * 512, 512)
         with jax.named_scope(f"split{half}"):
-            loads[1 + half].wait()
-            cols = pl.ds(half * 512, 512)
-            sub_tok[:, cols] = dot(tokens[...], ws[half]).astype(jnp.bfloat16)
+            for q in (2 * half, 2 * half + 1):
+                loads[1 + q].wait()
+                if q == 0:
+                    loads[3].start()
+                    loads[4].start()
+                if q == 2:
+                    loads[5].start()
+                    loads[6].start()
+                for m in range(2):
+                    top = pl.ds(m * 128, 128)
+                    sub_tok[top, pl.ds(q * 256, 256)] = dot(tokens[top, :], ws[q]).astype(jnp.bfloat16)
         with jax.named_scope(f"pack{half}"):
-            if half == 1:
-                for cp in loads[3:]:
-                    cp.start()
             for j in range(4):
                 rows_j = dot(chosen[pl.ds(j * 256, 256)], sub_tok[:, cols]).astype(jnp.bfloat16)
                 packed[pl.ds(j * 32, 32), :, cols] = rows_j.reshape(32, PAD, 512)
@@ -171,6 +182,8 @@
     with jax.named_scope("send_rest"):
         for i in range(EARLY, PEERS - 1):
             out_to(row(packed, i), row(recv, i), i)
+    for cp in loads[7:]:
+        cp.start()
     recv[PEERS - 1] = packed[PEERS - 1]
 
     with jax.named_scope("comb"):
@@ -185,8 +198,8 @@
             c = jnp.where(p == l0, v0, jnp.where(p == l1, v1, 0.0))
             comb[:, pl.ds(j * 256, 256)] = c.astype(jnp.bfloat16)
 
-    loads[3].wait()
-    loads[4].wait()
+    loads[5].wait()
+    loads[6].wait()
 
     def landed(ref, sem, j):
         lo, hi = EDGES[j], min(EDGES[j + 1], PEERS - 1)
@@ -218,7 +231,7 @@
     ret[PEERS - 1] = ans[PEERS - 1]
 
     for n in range(4):
-        loads[5 + n].wait()
+        loads[7 + n].wait()
     for j in range(PARTS):
         lo, n_rows = EDGES[j], (EDGES[j + 1] - EDGES[j]) * PAD
         with jax.named_scope(f"rwait{j}"):
@@ -235,57 +248,78 @@
     across = (ys[0] + zh[0] + xs[0], (2 - zw[0]) + cs[0])
 
     def send(src, dst, ss, rs, b, to):
+        cols = pl.ds(*BLOCKS[b])
         return pltpu.make_async_remote_copy(
-            src_ref=src.at[b], dst_ref=dst.at[b], send_sem=ss.at[b], recv_sem=rs.at[b],
+            src_ref=src.at[:, cols], dst_ref=dst.at[:, cols], send_sem=ss.at[b], recv_sem=rs.at[b],
             device_id=to, device_id_type=MESH,
         )
 
+    def send_dd(b):
+        return send(dd_s, dd_r, dd_ss, dd_rs, b, partner)
+
+    def send_f(b):
+        return send(f_s, f_r, f_ss, f_rs, b, partner)
+
     def send_z(b):
-        return pltpu.make_async_remote_copy(
-            src_ref=z_s.at[b], dst_ref=z_r.at[:, pl.ds(b * 256, 256)], send_sem=z_ss.at[b], recv_sem=z_rs.at[b],
-            device_id=across, device_id_type=MESH,
-        )
-
-    def product(n, b, width=256):
-        return dot(headb[...], wm[n, :, pl.ds(b * 256, width)])
+        return send(z_s, z_r, z_ss, z_rs, b, across)
+
+    tops = (pl.ds(0, 128), pl.ds(128, 128))
+
+    def product(n, b, top):
+        return dot(headb[top, :], wm[n, :, pl.ds(*BLOCKS[b])])
 
     def first(b):
-        dd_s[b] = product(0, b).astype(jnp.bfloat16)
-        send(dd_s, dd_r, dd_ss, dd_rs, b, partner).start()
+        for top in tops:
+            dd_s[top, pl.ds(*BLOCKS[b])] = product(0, b, top).astype(jnp.bfloat16)
+        send_dd(b).start()
+
+    def own(b):
+        for top in tops:
+            head[top, pl.ds(*BLOCKS[b])] = product(1, b, top)
 
     def second(b):
-        mine = product(1, b)
-        send(dd_s, dd_r, dd_ss, dd_rs, b, partner).wait_recv()
-        z_s[b] = (mine + dd_r[b].astype(jnp.float32)).astype(jnp.bfloat16)
+        cols = pl.ds(*BLOCKS[b])
+        send_dd(b).wait_recv()
+        z_s[:, cols] = (head[:, cols] + dd_r[:, cols].astype(jnp.float32)).astype(jnp.bfloat16)
         send_z(b).start()
 
+    blocks = range(len(BLOCKS))
     with jax.named_scope("merge"):
         first(0)
+        own(0)
         first(1)
+        own(1)
         second(0)
         first(2)
         second(1)
+        own(2)
         first(3)
         second(2)
+        own(3)
+        first(4)
         second(3)
+        own(4)
+        second(4)
     with jax.named_scope("merge_near"):
-        for b in range(4):
-            f_s[b] = product(2, b).astype(jnp.bfloat16)
-            send(f_s, f_r, f_ss, f_rs, b, partner).start()
+        for b in blocks:
+            for top in tops:
+                f_s[top, pl.ds(*BLOCKS[b])] = product(2, b, top).astype(jnp.bfloat16)
+            send_f(b).start()
         for b in range(2):
-            keep[:, pl.ds(b * 512, 512)] = product(3, 2 * b, 512)
-        for b in range(4):
-            send(f_s, f_r, f_ss, f_rs, b, partner).wait_recv()
-            keep[:, pl.ds(b * 256, 256)] += f_r[b].astype(jnp.float32)
+            keep[:, pl.ds(b * 512, 512)] = dot(headb[...], wm[3, :, pl.ds(b * 512, 512)])
+        for b in blocks:
+            cols = pl.ds(*BLOCKS[b])
+            send_f(b).wait_recv()
+            keep[:, cols] += f_r[:, cols].astype(jnp.float32)
         pltpu.make_async_copy(rows(packed, 0, PEERS - 1), rows(packed, 0, PEERS - 1), ds_sem).wait()
         pltpu.make_async_copy(rows(ans, 0, PEERS - 1), rows(ans, 0, PEERS - 1), rs_sem).wait()
-        for b in range(4):
-            send(dd_s, dd_r, dd_ss, dd_rs, b, partner).wait_send()
-            send(f_s, f_r, f_ss, f_rs, b, partner).wait_send()
+        for b in blocks:
+            send_dd(b).wait_send()
+            send_f(b).wait_send()
     with jax.named_scope("final"):
-        for b in range(4):
+        for b in blocks:
             send_z(b).wait_send()
-        for b in range(4):
+        for b in blocks:
             send_z(b).wait_recv()
 
 
@@ -294,7 +328,8 @@
     hbm = pl.BlockSpec(memory_space=pl.ANY)
     vm = pl.BlockSpec(memory_space=pltpu.VMEM)
     dma = pltpu.SemaphoreType.DMA
-    quarter = pltpu.VMEM((4, 256, 256), bf)
+    quarter = pltpu.VMEM((256, 1024), bf)
+    per_block = dma((len(BLOCKS),))
     slots = pltpu.VMEM((PEERS, PAD, 1024), bf)
     mine, other = pl.pallas_call(
         kernel,
@@ -307,7 +342,7 @@
             pltpu.VMEM((1, 128), i32),
             pltpu.VMEM((1, 128), i32),
             pltpu.VMEM((256, 4096), bf),
-            pltpu.VMEM((2, 4096, 512), bf),
+            pltpu.VMEM((4, 4096, 256), bf),
             pltpu.VMEM((4, 1024, 1024), bf),
             pltpu.VMEM((1024, 2048), bf),
             pltpu.VMEM((1024, 1024), bf),
@@ -322,8 +357,8 @@
             pltpu.VMEM((256, 1024), f32),
             pltpu.VMEM((256, 1024), bf),
             quarter, quarter, quarter, quarter, quarter,
-            dma((4,)), dma((5,)), dma((4,)), dma, dma((PARTS,)), dma, dma((PARTS,)),
-            dma((4,)), dma((4,)), dma((4,)), dma((4,)), dma((4,)), dma((4,)),
+            dma((4,)), dma((7,)), dma((4,)), dma, dma((PARTS,)), dma, dma((PARTS,)),
+            per_block, per_block, per_block, per_block, per_block, per_block,
         ],
         compiler_params=pltpu.CompilerParams(
             collective_id=0, has_side_effects=True, vmem_limit_bytes=58 * 2**20

time: 64.8 us -> 63.7 us (0.983)
  Pallas kernels: 63.8 us -> 62.6 us
    pallas_call x1, Pallas kernels: 63.8 us -> 62.6 us  [body(): pl.pallas_call(kernel, out_shape=[pltpu.VMEM((256, 1024), f32), pltpu.VME...]
where the time goes in v3:
time: 63.7 us; the launch traced here: 63.6 us
  Pallas kernels  62.6 us (98%)
  other arithmetic  0.94 us (1%)
    pallas_call x1, Pallas kernels, body(): pl.pallas_call(kernel, out_shape=[pltpu.VMEM((256, 1024), f32), pltpu.VME...  62.6 us

profile of v3, /device:TPU:1, one launch (start us, length us, event | category | flops | bytes accessed | tf_op | source)
XLA Modules:
  0.0 63.6 jit_solution(17851037112347387983)
XLA Ops:
  0.0 62.6 %shard_map.91 = (f32[256,1024]{1,0:T(8,128)S(1)}, bf16[256,1024]{1,0:T(8,128)(2,1)S(1)}) custom-call(s32[2,256]{1,0:T(2,128)} %bitcast.11, s32[2,256]{1,0:T(2,128)} %bitcast.12, s32[1,128]{1,0:T(1,128)} %bitcast.13, s32[1,128]{1,0:T(1,128)} %constant.7.table_h, bf16[256,4096]{1,0:T(8,128)(2,1)} %tokens_h.1, bf16[4096,1024]{1,0:T(8,128)(2,1)} %ws_h.1, ...), custom_call_target="tpu_custom_call" | custom-call | tf_op jit(solution)/shard_map/pallas_call | solution.py:334
  62.6 0.9 %add_convert_fusion = bf16[256,1024]{1,0:T(8,128)(2,1)} fusion(f32[256,1024]{1,0:T(8,128)S(1)} %get-tuple-element.7, bf16[256,1024]{1,0:T(8,128)(2,1)S(1)} %get-tuple-element.8), kind=kLoop, calls=%fused_computation | loop fusion | flops 786432 | bytes 2097152 | tf_op jit(solution)/shard_map/convert_element_type | solution.py:377

commit v4 on v3

--- a/solution.py
+++ b/solution.py
@@ -26,7 +26,9 @@
 
 
 def mixed():
-    return [(i * MUL) % PEERS for i in range(1, PEERS)] + [0]
+    steps = [(i * MUL) % PEERS for i in range(1, PEERS)]
+    runs = [steps[k : k + 32] for k in range(0, PEERS - 1, 32)]
+    return [r for run in runs for r in sorted(run, key=lambda r: -hops(r))] + [0]
 
 
 ORDER = mixed()

time: 63.7 us -> 62.8 us (0.986)
  Pallas kernels: 62.6 us -> 61.7 us
    pallas_call x1, Pallas kernels: 62.6 us -> 61.7 us  [body(): pl.pallas_call(kernel, out_shape=[pltpu.VMEM((256, 1024), f32), pltpu.VME...]
where the time goes in v4:
time: 62.8 us; the launch traced here: 62.7 us
  Pallas kernels  61.7 us (98%)
  other arithmetic  0.94 us (1%)
    pallas_call x1, Pallas kernels, body(): pl.pallas_call(kernel, out_shape=[pltpu.VMEM((256, 1024), f32), pltpu.VME...  61.7 us

profile of v4, /device:TPU:1, one launch (start us, length us, event | category | flops | bytes accessed | tf_op | source)
XLA Modules:
  0.0 62.7 jit_solution(4900950113461098569)
XLA Ops:
  0.0 61.7 %shard_map.91 = (f32[256,1024]{1,0:T(8,128)S(1)}, bf16[256,1024]{1,0:T(8,128)(2,1)S(1)}) custom-call(s32[2,256]{1,0:T(2,128)} %bitcast.11, s32[2,256]{1,0:T(2,128)} %bitcast.12, s32[1,128]{1,0:T(1,128)} %bitcast.13, s32[1,128]{1,0:T(1,128)} %constant.7.table_h, bf16[256,4096]{1,0:T(8,128)(2,1)} %tokens_h.1, bf16[4096,1024]{1,0:T(8,128)(2,1)} %ws_h.1, ...), custom_call_target="tpu_custom_call" | custom-call | tf_op jit(solution)/shard_map/pallas_call | solution.py:336
  61.7 0.9 %add_convert_fusion = bf16[256,1024]{1,0:T(8,128)(2,1)} fusion(f32[256,1024]{1,0:T(8,128)S(1)} %get-tuple-element.7, bf16[256,1024]{1,0:T(8,128)(2,1)S(1)} %get-tuple-element.8), kind=kLoop, calls=%fused_computation | loop fusion | flops 786432 | bytes 2097152 | tf_op jit(solution)/shard_map/convert_element_type | solution.py:379

commit v5 on v4

--- a/solution.py
+++ b/solution.py
@@ -11,7 +11,7 @@
 SLOTS = 6
 PAD = 8
 EDGES = (0, 32, 64, 96, 128)
-EARLY = 40
+EARLY = 32
 MUL = 45
 BLOCKS = ((0, 128), (128, 128), (256, 256), (512, 256), (768, 256))
 PARTS = len(EDGES) - 1

time: 62.8 us -> 62.7 us (level)
  no operation moved by 1% of the time
where the time goes in v5:
time: 62.7 us; the launch traced here: 62.6 us
  Pallas kernels  61.6 us (98%)
  other arithmetic  0.94 us (1%)
    pallas_call x1, Pallas kernels, body(): pl.pallas_call(kernel, out_shape=[pltpu.VMEM((256, 1024), f32), pltpu.VME...  61.6 us

profile of v5, /device:TPU:1, one launch (start us, length us, event | category | flops | bytes accessed | tf_op | source)
XLA Modules:
  0.0 62.6 jit_solution(8520849380261893492)
XLA Ops:
  0.0 61.6 %shard_map.91 = (f32[256,1024]{1,0:T(8,128)S(1)}, bf16[256,1024]{1,0:T(8,128)(2,1)S(1)}) custom-call(s32[2,256]{1,0:T(2,128)} %bitcast.11, s32[2,256]{1,0:T(2,128)} %bitcast.12, s32[1,128]{1,0:T(1,128)} %bitcast.13, s32[1,128]{1,0:T(1,128)} %constant.7.table_h, bf16[256,4096]{1,0:T(8,128)(2,1)} %tokens_h.1, bf16[4096,1024]{1,0:T(8,128)(2,1)} %ws_h.1, ...), custom_call_target="tpu_custom_call" | custom-call | tf_op jit(solution)/shard_map/pallas_call | solution.py:336
  61.6 0.9 %add_convert_fusion = bf16[256,1024]{1,0:T(8,128)(2,1)} fusion(f32[256,1024]{1,0:T(8,128)S(1)} %get-tuple-element.7, bf16[256,1024]{1,0:T(8,128)(2,1)S(1)} %get-tuple-element.8), kind=kLoop, calls=%fused_computation | loop fusion | flops 786432 | bytes 2097152 | tf_op jit(solution)/shard_map/convert_element_type | solution.py:379
